TPU v7x, 32 devices: a whole 2x2x4 slice. The times are simulated.
32 devices in a mesh: row: 8 (over z, y), col: 4 (over x, core).
Axes of the slice: x: 2, y: 2, z: 4, core: 2. Of those that a mesh axis runs over, the one named last changes fastest.
Arguments:
- expression: bfloat16 [4096, 1024], P(('row', 'col')), as said below
- power_order: int32 [20], replicated, may hold values from 0 to 19, each once
Outputs:
- log_conn: float32 [4096, 20], P(('row', 'col'))
- fit: float32 [20], replicated
- slope: float32 [20], replicated
Inputs may be any that keep to these rules, and one draw needn't show every extreme that they name: `expression`: each gene's row has mean zero and unit variance over the samples, up to rounding.
All inputs are finite; a program needn't handle non-finite values.
Results may differ from a plain program's by a relative error of at most 0.0029.
Values may be sent and summed in bfloat16 or wider, within the bound.
No kernel may reach another device: no remote copies, remote signals or barrier semaphores. Data moves between devices by JAX's collectives and lax.ppermute only.
A program may use at most 64 MiB of HBM per device.

v0:
```python
import math
import jax
import jax.numpy as jnp
from jax import lax
from jax.sharding import PartitionSpec as P


def power_sums(rows, partners, samples, powers):
    corr = (
        lax.dot_general(
            rows, partners, (((1,), (1,)), ((), ())), preferred_element_type=jnp.float32
        )
        / samples
    )
    magnitude = jnp.abs(corr)
    current = magnitude
    sums = []
    for power in range(powers):
        sums.append(jnp.sum(current, axis=1))
        current = current * magnitude
    return jnp.stack(sums, axis=1)


def scale_free_fit(hist, log_total, bins):
    centers = jnp.arange(bins, dtype=jnp.float32) * (log_total / (bins - 1))
    weight_sum = jnp.sum(hist, axis=1, keepdims=True)
    ylog = jnp.log(hist + 1.0) - log_total
    xmean = jnp.sum(hist * centers[None, :], axis=1, keepdims=True) / weight_sum
    ymean = jnp.sum(hist * ylog, axis=1, keepdims=True) / weight_sum
    xdev = centers[None, :] - xmean
    ydev = ylog - ymean
    sxx = jnp.maximum(jnp.sum(hist * xdev * xdev, axis=1) / weight_sum[:, 0], 0.05)
    syy = jnp.maximum(jnp.sum(hist * ydev * ydev, axis=1) / weight_sum[:, 0], 0.05)
    sxy = jnp.sum(hist * xdev * ydev, axis=1) / weight_sum[:, 0]
    return (-sxy * jnp.abs(sxy) / (sxx * syy), sxy / sxx)


def on_device(expression, power_order):
    samples = expression.shape[1]
    powers = power_order.shape[0]
    bins = 128
    genes_total = expression.shape[0] * lax.axis_size("row") * lax.axis_size("col")
    panel = lax.all_gather(expression, "col", axis=0, tiled=True)
    partial_value = power_sums(
        panel, lax.all_gather(expression, "row", axis=0, tiled=True), samples, powers
    )
    conn = lax.psum_scatter(partial_value, "col", scatter_dimension=0, tiled=True)
    selector = (power_order[:, None] == jnp.arange(powers, dtype=jnp.int32)[None, :]).astype(
        jnp.float32
    )
    picked = jnp.dot(conn, selector.T, precision=lax.Precision.HIGHEST)
    log_conn = jnp.log(picked)
    log_total = math.log(genes_total)
    position = log_conn * ((bins - 1) / log_total)
    levels = jnp.arange(bins, dtype=jnp.float32)
    weights = jnp.maximum(0.0, 1.0 - jnp.abs(position[:, :, None] - levels[None, None, :]))
    local_hist = jnp.sum(weights, axis=0)
    hist = lax.psum(local_hist, ("row", "col"))
    fit, slope = scale_free_fit(hist, log_total, bins)
    return (log_conn, fit, slope)


def solution(mesh):
    placed = (P(("row", "col"), None), P())
    return jax.shard_map(
        on_device,
        mesh=mesh,
        in_specs=placed,
        out_specs=(P(("row", "col"), None), P(), P()),
        check_vma=False,
    )
```

profile of v0, /device:TPU:0, one launch (start us, length us, event | category | flops | bytes accessed | tf_op | source)
XLA Modules:
  0.0 156.3 jit_solution(5682563446341147419)
XLA Ops:
  7.2 0.0 all-gather.3.cloned.1.call-start
  7.2 0.7 all-gather.3.cloned.1.call-update
  7.9 0.0 all-gather.5.cloned.1.call-start
  7.9 0.7 all-gather.5.cloned.1.call-update
  8.6 0.0 copy-start
  8.7 0.0 reduce-scatter.2.cloned.1.call-start
  8.7 20.3 %all-gather.3.cloned.1.call-done = bf16[512,1024]{1,0:T(8,128)(2,1)} async-done(((bf16[128,1024]{1,0:T(8,128)(2,1)}), bf16[512,1024]{1,0:T(8,128)(2,1)}) %all-gather.3.cloned.1.call-update) | async-done | bytes 1048592 | tf_op jit(solution)/shard_map/all_gather | solution.py:43
  29.0 51.3 %all-gather.5.cloned.1.call-done = bf16[1024,1024]{1,0:T(8,128)(2,1)} async-done(((bf16[128,1024]{1,0:T(8,128)(2,1)}), bf16[1024,1024]{1,0:T(8,128)(2,1)}) %all-gather.5.cloned.1.call-update) | async-done | bytes 2097168 | tf_op jit(solution)/shard_map/all_gather | solution.py:45
  80.2 6.5 %multiply_reduce_fusion = (f32[512]{0:T(512)S(1)}, f32[512]{0:T(512)S(1)}, f32[512]{0:T(512)S(1)}, f32[512]{0:T(512)S(1)}, f32[512]{0:T(512)S(1)}, /*index=5*/f3...) fusion(bf16[512,1024]{1,0:T(8,128)(2,1)} %all-gather.3.cloned.1, ...), kind=kOutput, calls=%fused_computation | convolution fusion | flops 1095227392 | bytes 3186688 | tf_op jit(solution)/shard_map/dot_general | solution.py:10
  86.8 1.9 %stack.83 = f32[512,20]{0,1:T(8,128)} concatenate(f32[512,1]{0,1:T(1,128)S(1)} %bitcast.42, f32[512,1]{0,1:T(1,128)S(1)} %bitcast.41, f32[512,1]{0,1:T(1,128)S(1)} %bitcast.39, f32[512,1]{0,1:T(1,128)S(1)} %bitcast.40, f32[512,1]{0,1:T(1,128)S(1)} %bitcast.35, f32[512,1]{0,1:T(1,128)S(1)} %bitcast.36, f32[512,1]{0,1:T(1,128)S(1)} %bitcast.38, f32[512,1]{0,1:T(1,128)S(1)} %bitcast.37, ...), dimensions={1} | concatenate | bytes 81920 | tf_op jit(solution)/shard_map/stack | solution.py:21
  88.7 0.0 reduce-scatter.2.cloned.1.call-update
  88.7 18.2 %reduce-scatter.2.cloned.1.call-done = f32[128,20]{0,1:T(8,128)} async-done(((f32[512,20]{0,1:T(8,128)}), f32[128,20]{0,1:T(8,128)}) %reduce-scatter.2.cloned.1.call-update) | async-done | bytes 10256 | tf_op jit(solution)/shard_map/reduce_scatter | solution.py:47
  106.9 0.0 copy-done
  106.9 1.5 broadcast_multiply_fusion
  108.4 0.4 maximum_reduce_fusion
  108.8 39.5 %psum.7 = f32[20,128]{1,0:T(8,128)S(1)} all-reduce(f32[20,128]{1,0:T(8,128)S(1)} %maximum_reduce_fusion), channel_id=1, replica_groups=mesh['row'=8,'col'=4] {'row','col'}, use_global_device_ids=true, to_apply=%region_22.0 | all-reduce | flops 2560 | bytes 20480 | tf_op jit(solution)/shard_map/psum | solution.py:58
  148.3 0.2 multiply_reduce_fusion.11
  148.5 0.2 multiply_reduce_fusion.10
  148.7 0.5 multiply_divide_fusion
  149.2 0.5 multiply_divide_fusion.1
  (2 shorter events, 0.0 us)
Async XLA Ops:
  7.2 21.8 %all-gather.3.cloned.1.call-start = ((), (), s32[]{:S(2)}) async-start(), calls=%async_computation.1 | async-start | bytes 1310720 | tf_op jit(solution)/shard_map/all_gather | solution.py:43
  7.9 72.3 %all-gather.5.cloned.1.call-start = ((), (), s32[]{:S(2)}) async-start(), calls=%async_computation.2 | async-start | bytes 2359296 | tf_op jit(solution)/shard_map/all_gather | solution.py:45
  8.6 98.3 %copy-start = (s32[20]{0:T(128)S(1)}, s32[20]{0:T(128)}, u32[]{:S(2)}) copy-start(s32[20]{0:T(128)} %param.3) | copy-start | bytes 244
  8.7 98.2 %reduce-scatter.2.cloned.1.call-start = ((), (), s32[]{:S(2)}) async-start(), calls=%async_computation.3 | async-start | bytes 61440 | tf_op jit(solution)/shard_map/reduce_scatter | solution.py:47
Sparse Core Ops, SparseCore 0:
  9.5 19.4 all-gather.2
  31.1 49.0 all-gather.4
  88.8 18.0 reduce-scatter.1
where the time goes:
time: 157 us; the launch traced here: 156 us
  waiting for transfers between devices  91.1 us (58%)
  blocking collectives  39.5 us (25%)
  between operations  13.8 us (9%)
  matrix products  8.05 us (5%)
  local copies, waits for them, and re-layouts  1.88 us (1%)
  other arithmetic  1.88 us (1%)
    all_gather x1, waiting for transfers between devices, on_device(): lax.all_gather(expression, 'row', axis=0, tiled=True)  51.3 us
    psum x1, blocking collectives, on_device(): hist = lax.psum(local_hist, ('row', 'col'))  39.5 us
    all_gather x1, waiting for transfers between devices, on_device(): panel = lax.all_gather(expression, 'col', axis=0, tiled=True)  20.3 us
    reduce_scatter x1, waiting for transfers between devices, on_device(): lax.psum_scatter(partial_value, 'col', scatter_dimension=0, tiled=True)  18.2 us
    dot_general x1, matrix products, power_sums(): lax.dot_general(rows, partners, (((1,), (1,)), ((), ())), preferred_eleme...  6.54 us
  transfers between devices with their start and end apart: 3, of which 3 were waited for; matrix products, arithmetic and copies ran while one was open for 0% of the time, Pallas kernels for 0%

commit v1 on v0

--- a/solution.py
+++ b/solution.py
@@ -55,7 +55,7 @@
     levels = jnp.arange(bins, dtype=jnp.float32)
     weights = jnp.maximum(0.0, 1.0 - jnp.abs(position[:, :, None] - levels[None, None, :]))
     local_hist = jnp.sum(weights, axis=0)
-    hist = lax.psum(local_hist, ("row", "col"))
+    hist = lax.psum(lax.psum(local_hist, "col"), "row")
     fit, slope = scale_free_fit(hist, log_total, bins)
     return (log_conn, fit, slope)
 

time: 157 us -> 164 us (1.045)
  blocking collectives: 39.5 us -> 47.3 us
    psum x1 -> x2, blocking collectives: 39.5 us -> 47.3 us  [on_device(): hist = lax.psum(lax.psum(local_hist, 'col'), 'row')]
where the time goes in v1:
time: 164 us
  waiting for transfers between devices  91.1 us (56%)
  blocking collectives  47.3 us (29%)
  between operations  13.8 us (8%)
  matrix products  8.05 us (5%)
  local copies, waits for them, and re-layouts  1.88 us (1%)
  other arithmetic  1.88 us (1%)
    all_gather x1, waiting for transfers between devices, on_device(): lax.all_gather(expression, 'row', axis=0, tiled=True)  51.3 us
    psum x2, blocking collectives, on_device(): hist = lax.psum(lax.psum(local_hist, 'col'), 'row')  47.3 us
    all_gather x1, waiting for transfers between devices, on_device(): panel = lax.all_gather(expression, 'col', axis=0, tiled=True)  20.3 us
    reduce_scatter x1, waiting for transfers between devices, on_device(): lax.psum_scatter(partial_value, 'col', scatter_dimension=0, tiled=True)  18.2 us
    dot_general x1, matrix products, power_sums(): lax.dot_general(rows, partners, (((1,), (1,)), ((), ())), preferred_eleme...  6.54 us
  transfers between devices with their start and end apart: 3, of which 3 were waited for; matrix products, arithmetic and copies ran while one was open for 0% of the time, Pallas kernels for 0%

profile of v1, /device:TPU:0, one launch (start us, length us, event | category | flops | bytes accessed | tf_op | source)
XLA Modules:
  0.0 164.1 jit_solution(18399924165479159366)
XLA Ops:
  7.2 0.0 all-gather.3.cloned.1.call-start
  7.2 0.7 all-gather.3.cloned.1.call-update
  7.9 0.0 all-gather.5.cloned.1.call-start
  7.9 0.7 all-gather.5.cloned.1.call-update
  8.6 0.0 copy-start
  8.7 0.0 reduce-scatter.2.cloned.1.call-start
  8.7 20.3 %all-gather.3.cloned.1.call-done = bf16[512,1024]{1,0:T(8,128)(2,1)} async-done(((bf16[128,1024]{1,0:T(8,128)(2,1)}), bf16[512,1024]{1,0:T(8,128)(2,1)}) %all-gather.3.cloned.1.call-update) | async-done | bytes 1048592 | tf_op jit(solution)/shard_map/all_gather | solution.py:43
  29.0 51.3 %all-gather.5.cloned.1.call-done = bf16[1024,1024]{1,0:T(8,128)(2,1)} async-done(((bf16[128,1024]{1,0:T(8,128)(2,1)}), bf16[1024,1024]{1,0:T(8,128)(2,1)}) %all-gather.5.cloned.1.call-update) | async-done | bytes 2097168 | tf_op jit(solution)/shard_map/all_gather | solution.py:45
  80.2 6.5 %multiply_reduce_fusion = (f32[512]{0:T(512)S(1)}, f32[512]{0:T(512)S(1)}, f32[512]{0:T(512)S(1)}, f32[512]{0:T(512)S(1)}, f32[512]{0:T(512)S(1)}, /*index=5*/f3...) fusion(bf16[512,1024]{1,0:T(8,128)(2,1)} %all-gather.3.cloned.1, ...), kind=kOutput, calls=%fused_computation | convolution fusion | flops 1095227392 | bytes 3186688 | tf_op jit(solution)/shard_map/dot_general | solution.py:10
  86.8 1.9 %stack.83 = f32[512,20]{0,1:T(8,128)} concatenate(f32[512,1]{0,1:T(1,128)S(1)} %bitcast.42, f32[512,1]{0,1:T(1,128)S(1)} %bitcast.41, f32[512,1]{0,1:T(1,128)S(1)} %bitcast.39, f32[512,1]{0,1:T(1,128)S(1)} %bitcast.40, f32[512,1]{0,1:T(1,128)S(1)} %bitcast.35, f32[512,1]{0,1:T(1,128)S(1)} %bitcast.36, f32[512,1]{0,1:T(1,128)S(1)} %bitcast.38, f32[512,1]{0,1:T(1,128)S(1)} %bitcast.37, ...), dimensions={1} | concatenate | bytes 81920 | tf_op jit(solution)/shard_map/stack | solution.py:21
  88.7 0.0 reduce-scatter.2.cloned.1.call-update
  88.7 18.2 %reduce-scatter.2.cloned.1.call-done = f32[128,20]{0,1:T(8,128)} async-done(((f32[512,20]{0,1:T(8,128)}), f32[128,20]{0,1:T(8,128)}) %reduce-scatter.2.cloned.1.call-update) | async-done | bytes 10256 | tf_op jit(solution)/shard_map/reduce_scatter | solution.py:47
  106.9 0.0 copy-done
  106.9 1.5 broadcast_multiply_fusion
  108.4 0.4 maximum_reduce_fusion
  108.8 10.1 %psum.14 = f32[20,128]{1,0:T(8,128)S(1)} all-reduce(f32[20,128]{1,0:T(8,128)S(1)} %maximum_reduce_fusion), channel_id=1, replica_groups=mesh['row'=8,'col'=4] {'col'}, use_global_device_ids=true, to_apply=%region_22.0 | all-reduce | flops 2560 | bytes 20480 | tf_op jit(solution)/shard_map/psum | solution.py:58
  119.0 37.1 %psum.15 = f32[20,128]{1,0:T(8,128)S(1)} all-reduce(f32[20,128]{1,0:T(8,128)S(1)} %psum.14), channel_id=1, replica_groups=mesh['row'=8,'col'=4] {'row'}, use_global_device_ids=true, to_apply=%region_23.0 | all-reduce | flops 2560 | bytes 20480 | tf_op jit(solution)/shard_map/psum | solution.py:58
  156.1 0.2 multiply_reduce_fusion.11
  156.3 0.2 multiply_reduce_fusion.10
  156.5 0.5 multiply_divide_fusion
  157.0 0.5 multiply_divide_fusion.1
  (2 shorter events, 0.0 us)
Async XLA Ops:
  7.2 21.8 %all-gather.3.cloned.1.call-start = ((), (), s32[]{:S(2)}) async-start(), calls=%async_computation.1 | async-start | bytes 1310720 | tf_op jit(solution)/shard_map/all_gather | solution.py:43
  7.9 72.3 %all-gather.5.cloned.1.call-start = ((), (), s32[]{:S(2)}) async-start(), calls=%async_computation.2 | async-start | bytes 2359296 | tf_op jit(solution)/shard_map/all_gather | solution.py:45
  8.6 98.3 %copy-start = (s32[20]{0:T(128)S(1)}, s32[20]{0:T(128)}, u32[]{:S(2)}) copy-start(s32[20]{0:T(128)} %param.3) | copy-start | bytes 244
  8.7 98.2 %reduce-scatter.2.cloned.1.call-start = ((), (), s32[]{:S(2)}) async-start(), calls=%async_computation.3 | async-start | bytes 61440 | tf_op jit(solution)/shard_map/reduce_scatter | solution.py:47
Sparse Core Ops, SparseCore 0:
  9.5 19.4 all-gather.2
  31.1 49.0 all-gather.4
  88.8 18.0 reduce-scatter.1

commit v2 on v0

--- a/solution.py
+++ b/solution.py
@@ -40,7 +40,12 @@
     powers = power_order.shape[0]
     bins = 128
     genes_total = expression.shape[0] * lax.axis_size("row") * lax.axis_size("col")
-    panel = lax.all_gather(expression, "col", axis=0, tiled=True)
+    ring = [expression]
+    for hop in range(3):
+        ring.append(lax.ppermute(ring[-1], "col", [(dev, (dev + 1) % 4) for dev in range(4)]))
+    panel = jnp.roll(
+        jnp.concatenate(ring[::-1], axis=0), (lax.axis_index("col") + 1) * ring[0].shape[0], axis=0
+    )
     partial_value = power_sums(
         panel, lax.all_gather(expression, "row", axis=0, tiled=True), samples, powers
     )

time: 157 us -> 139 us (0.89)
  waiting for transfers between devices: 91.1 us -> 71.1 us
    all_gather x1 -> x0, waiting for transfers between devices: 20.3 us -> none  [on_device(): panel = lax.all_gather(expression, 'col', axis=0, tiled=True)]
    ppermute x0 -> x3, waiting for transfers between devices: none -> 17.7 us  [on_device(): lax.ppermute(ring[-1], 'col', [(dev, (dev + 1) % 4) for dev in range(4)])]
    all_gather x1, waiting for transfers between devices: 51.3 us -> 34.5 us  [on_device(): lax.all_gather(expression, 'row', axis=0, tiled=True)]
  transfers between devices with their start and end apart: 3 -> 5, of which waited for: 3 -> 5; matrix products, arithmetic and copies ran while one was open for 0% -> 1% of each run, Pallas kernels for 0% -> 0%
where the time goes in v2:
time: 139 us; the launch traced here: 138 us
  waiting for transfers between devices  71.1 us (51%)
  blocking collectives  39.5 us (28%)
  between operations  14.1 us (10%)
  matrix products  8.05 us (6%)
  local copies, waits for them, and re-layouts  2.99 us (2%)
  other arithmetic  1.88 us (1%)
    psum x1, blocking collectives, on_device(): hist = lax.psum(local_hist, ('row', 'col'))  39.5 us
    all_gather x1, waiting for transfers between devices, on_device(): lax.all_gather(expression, 'row', axis=0, tiled=True)  34.5 us
    reduce_scatter x1, waiting for transfers between devices, on_device(): lax.psum_scatter(partial_value, 'col', scatter_dimension=0, tiled=True)  18.2 us
    ppermute x3, waiting for transfers between devices, on_device(): lax.ppermute(ring[-1], 'col', [(dev, (dev + 1) % 4) for dev in range(4)])  17.7 us
    dot_general x1, matrix products, power_sums(): lax.dot_general(rows, partners, (((1,), (1,)), ((), ())), preferred_eleme...  6.54 us
  transfers between devices with their start and end apart: 5, of which 5 were waited for; matrix products, arithmetic and copies ran while one was open for 1% of the time, Pallas kernels for 0%

profile of v2, /device:TPU:0, one launch (start us, length us, event | category | flops | bytes accessed | tf_op | source)
XLA Modules:
  0.0 138.3 jit_solution(11444439079924638947)
XLA Ops:
  7.2 0.0 copy-start
  7.2 0.0 all-gather.2.cloned.1.call-start
  7.2 0.7 all-gather.2.cloned.1.call-update
  7.9 0.0 reduce-scatter.2.cloned.1.call-start
  8.0 0.5 collective-permute-start
  8.5 6.2 %collective-permute-done = bf16[128,1024]{1,0:T(8,128)(2,1)S(1)} collective-permute-done((bf16[128,1024]{1,0:T(8,128)(2,1)}, bf16[128,1024]{1,0:T(8,128)(2,1)S(1)}, u32[]{:S(2)}, u32[]{:S(2)}) %collective-permute-start) | collective-permute-done | bytes 262176 | tf_op jit(solution)/shard_map/ppermute | solution.py:45
  14.7 0.0 collective-permute-start.1
  14.7 5.8 %collective-permute-done.1 = bf16[128,1024]{1,0:T(8,128)(2,1)S(1)} collective-permute-done((bf16[128,1024]{1,0:T(8,128)(2,1)S(1)}, bf16[128,1024]{1,0:T(8,128)(2,1)S(1)}, u32[]{:S(2)}, u32[]{:S(2)}) %collective-permute-start.1) | collective-permute-done | bytes 262176 | tf_op jit(solution)/shard_map/ppermute | solution.py:45
  20.5 0.0 collective-permute-start.2
  20.5 5.8 %collective-permute-done.2 = bf16[128,1024]{1,0:T(8,128)(2,1)S(1)} collective-permute-done((bf16[128,1024]{1,0:T(8,128)(2,1)S(1)}, bf16[128,1024]{1,0:T(8,128)(2,1)S(1)}, u32[]{:S(2)}, u32[]{:S(2)}) %collective-permute-start.2) | collective-permute-done | bytes 262176 | tf_op jit(solution)/shard_map/ppermute | solution.py:45
  26.4 1.0 constant_dynamic-update-slice_fusion.4
  27.4 0.0 copy-done
  27.4 0.0 copy-start.1
  27.5 34.5 %all-gather.2.cloned.1.call-done = bf16[1024,1024]{1,0:T(8,128)(2,1)} async-done(((bf16[128,1024]{1,0:T(8,128)(2,1)}), bf16[1024,1024]{1,0:T(8,128)(2,1)}) %all-gather.2.cloned.1.call-update) | async-done | bytes 2097168 | tf_op jit(solution)/shard_map/all_gather | solution.py:50
  62.0 6.5 %multiply_reduce_fusion = (f32[512]{0:T(512)S(1)}, f32[512]{0:T(512)S(1)}, f32[512]{0:T(512)S(1)}, f32[512]{0:T(512)S(1)}, f32[512]{0:T(512)S(1)}, /*index=5*/f3...) fusion(bf16[1024,1024]{1,0:T(8,128)(2,1)} %all-gather.2.cloned., ...), kind=kOutput, calls=%fused_computation | convolution fusion | flops 1095227392 | bytes 3186692 | tf_op jit(solution)/shard_map/dot_general | solution.py:10
  68.5 1.9 %stack.83 = f32[512,20]{0,1:T(8,128)} concatenate(f32[512,1]{0,1:T(1,128)S(1)} %bitcast.41, f32[512,1]{0,1:T(1,128)S(1)} %bitcast.40, f32[512,1]{0,1:T(1,128)S(1)} %bitcast.38, f32[512,1]{0,1:T(1,128)S(1)} %bitcast.39, f32[512,1]{0,1:T(1,128)S(1)} %bitcast.34, f32[512,1]{0,1:T(1,128)S(1)} %bitcast.35, f32[512,1]{0,1:T(1,128)S(1)} %bitcast.37, f32[512,1]{0,1:T(1,128)S(1)} %bitcast.36, ...), dimensions={1} | concatenate | bytes 81920 | tf_op jit(solution)/shard_map/stack | solution.py:21
  70.4 0.0 reduce-scatter.2.cloned.1.call-update
  70.4 18.2 %reduce-scatter.2.cloned.1.call-done = f32[128,20]{0,1:T(8,128)} async-done(((f32[512,20]{0,1:T(8,128)}), f32[128,20]{0,1:T(8,128)}) %reduce-scatter.2.cloned.1.call-update) | async-done | bytes 10256 | tf_op jit(solution)/shard_map/reduce_scatter | solution.py:52
  88.6 0.0 copy-done.1
  88.6 1.5 %broadcast_multiply_fusion = (f32[128,20]{0,1:T(8,128)S(1)}, f32[128,20]{0,1:T(8,128)}) fusion(f32[128,20]{0,1:T(8,128)} %reduce-scatter.2.cloned.1.call-done, s32[20]{0:T(128)S(1)} %copy-done.1), kind=kOutput, calls=%fused_computation.50 | convolution fusion | flops 617360 | bytes 30800 | tf_op jit(solution)/shard_map/dot_general | solution.py:56
  90.1 0.4 maximum_reduce_fusion
  90.6 39.5 %psum.7 = f32[20,128]{1,0:T(8,128)S(1)} all-reduce(f32[20,128]{1,0:T(8,128)S(1)} %maximum_reduce_fusion), channel_id=1, replica_groups=mesh['row'=8,'col'=4] {'row','col'}, use_global_device_ids=true, to_apply=%region_22.23 | all-reduce | flops 2560 | bytes 20480 | tf_op jit(solution)/shard_map/psum | solution.py:63
  130.0 0.2 multiply_reduce_fusion.11
  130.2 0.2 multiply_reduce_fusion.10
  130.4 0.5 multiply_divide_fusion
  131.0 0.5 multiply_divide_fusion.1
  (9 shorter events, 0.2 us)
Async XLA Ops:
  7.2 20.2 %copy-start = (bf16[128,1024]{1,0:T(8,128)(2,1)S(1)}, bf16[128,1024]{1,0:T(8,128)(2,1)}, u32[]{:S(2)}) copy-start(bf16[128,1024]{1,0:T(8,128)(2,1)} %param.2) | copy-start | bytes 786436
  7.2 54.8 %all-gather.2.cloned.1.call-start = ((), (), s32[]{:S(2)}) async-start(), calls=%async_computation.1 | async-start | bytes 2359296 | tf_op jit(solution)/shard_map/all_gather | solution.py:50
  7.9 80.7 %reduce-scatter.2.cloned.1.call-start = ((), (), s32[]{:S(2)}) async-start(), calls=%async_computation.2 | async-start | bytes 61440 | tf_op jit(solution)/shard_map/reduce_scatter | solution.py:52
  8.0 6.7 %collective-permute-start = (bf16[128,1024]{1,0:T(8,128)(2,1)}, bf16[128,1024]{1,0:T(8,128)(2,1)S(1)}, u32[]{:S(2)}, u32[]{:S(2)}) collective-permute-start(bf16[128,1024]{1,0:T(8,128)(2,1)} %param.2), channel_id=1, source_target_pairs={{0,1},{1,2},{2,3},{3,0},{4,5},{5,6},{6,7},{7,4},{8,9},{9,10},{10,1... | collective-permute-start | bytes 786440 | tf_op jit(solution)/shard_map/ppermute | solution.py:45
  14.7 5.8 %collective-permute-start.1 = (bf16[128,1024]{1,0:T(8,128)(2,1)S(1)}, bf16[128,1024]{1,0:T(8,128)(2,1)S(1)}, u32[]{:S(2)}, u32[]{:S(2)}) collective-permute-start(bf16[128,1024]{1,0:T(8,128)(2,1)S(1)} %collective-permute-done), channel_id=1, source_target_pairs={{0,1},{1,2},{2,3},{3,0},{4,5},{5,6},{6,7},{7,4},{8,9},{9,10},{10,1... | collective-permute-start | bytes 786440 | tf_op jit(solution)/shard_map/ppermute | solution.py:45
  20.5 5.8 %collective-permute-start.2 = (bf16[128,1024]{1,0:T(8,128)(2,1)S(1)}, bf16[128,1024]{1,0:T(8,128)(2,1)S(1)}, u32[]{:S(2)}, u32[]{:S(2)}) collective-permute-start(bf16[128,1024]{1,0:T(8,128)(2,1)S(1)} %collective-permute-done.1), channel_id=1, source_target_pairs={{0,1},{1,2},{2,3},{3,0},{4,5},{5,6},{6,7},{7,4},{8,9},{9,10},{10,1... | collective-permute-start | bytes 786440 | tf_op jit(solution)/shard_map/ppermute | solution.py:45
  27.4 61.2 %copy-start.1 = (s32[20]{0:T(128)S(1)}, s32[20]{0:T(128)}, u32[]{:S(2)}) copy-start(s32[20]{0:T(128)} %param.3) | copy-start | bytes 244
Sparse Core Ops, SparseCore 0:
  10.1 51.8 all-gather.1
  70.5 18.0 reduce-scatter.1
